TPU v7x, 8 devices: a whole 2x2x1 slice. The times are simulated.
8 devices in a mesh: ep: 8 (over z, y, x, core).
Axes of the slice: x: 2, y: 2, z: 1, core: 2. Of those that a mesh axis runs over, the one named last changes fastest.
Arguments:
- hidden: bfloat16 [1024, 2048], P('ep')
- w_router: float32 [2048, 8], replicated
- expert_ids: int32 [1024, 2], P('ep')
- w_one: bfloat16 [8, 2048, 5632], P('ep')
- w_three: bfloat16 [8, 2048, 5632], P('ep')
- w_two: bfloat16 [8, 5632, 2048], P('ep')
Outputs:
- output: bfloat16 [1024, 2048], P('ep')
All inputs are finite; a program needn't handle non-finite values.
Results may differ from a plain program's by a relative error of at most 0.00869076.
Values are sent between devices in bfloat16 or wider.
A program may use at most 1 GiB of HBM per device.

v0:
```python
import jax
import jax.numpy as jnp
from jax import lax
from jax.sharding import PartitionSpec as P


def route_gates(hidden_loc, w_router, ids_loc):
    logits = jnp.dot(hidden_loc.astype(jnp.float32), w_router, preferred_element_type=jnp.float32)
    prob_vals = jax.nn.softmax(logits, axis=-1)
    picked = jnp.take_along_axis(prob_vals, ids_loc, axis=1)
    return picked / jnp.sum(picked, axis=1, keepdims=True)


def expert_ffn(sorted_rows, group_sizes, w_one, w_three, w_two):
    h_one = lax.ragged_dot(sorted_rows, w_one, group_sizes, preferred_element_type=jnp.float32)
    h_three = lax.ragged_dot(sorted_rows, w_three, group_sizes, preferred_element_type=jnp.float32)
    act_rows = (jax.nn.silu(h_one) * h_three).astype(jnp.bfloat16)
    return lax.ragged_dot(act_rows, w_two, group_sizes, preferred_element_type=jnp.float32).astype(jnp.bfloat16)


def solution(mesh):
    dev_count = mesh.shape["ep"]

    def device_body(hidden_loc, w_router, ids_loc, w_one, w_three, w_two):
        tok_count = hidden_loc.shape[0]
        model_dim = hidden_loc.shape[1]
        local_count = w_one.shape[0]
        row_cap = 4 * tok_count // dev_count
        gate_vals = route_gates(hidden_loc, w_router, ids_loc)
        flat_ids = ids_loc.reshape(-1)
        assign_count = flat_ids.shape[0]
        dest_dev = flat_ids // local_count
        dest_onehot = (dest_dev[:, None] == jnp.arange(dev_count)[None, :]).astype(jnp.int32)
        slot_idx = jnp.sum(jnp.cumsum(dest_onehot, axis=0) * dest_onehot, axis=1) - 1
        slot_pos = dest_dev * row_cap + slot_idx
        src_token = jnp.zeros((dev_count * row_cap,), jnp.int32).at[slot_pos].set(jnp.arange(assign_count, dtype=jnp.int32) // 2)
        send_exp = jnp.full((dev_count * row_cap,), local_count, jnp.int32).at[slot_pos].set(flat_ids % local_count)
        send_rows = jnp.take(hidden_loc, src_token, axis=0).reshape(dev_count, row_cap, model_dim)
        recv_rows = lax.all_to_all(send_rows, "ep", 0, 0, tiled=True)
        recv_exp = lax.all_to_all(send_exp.reshape(dev_count, row_cap), "ep", 0, 0, tiled=True)
        row_exp = recv_exp.reshape(-1)
        sort_order = jnp.argsort(row_exp, stable=True)
        group_sizes = jnp.sum((row_exp[:, None] == jnp.arange(local_count)[None, :]).astype(jnp.int32), axis=0)
        sorted_rows = jnp.take(recv_rows.reshape(dev_count * row_cap, model_dim), sort_order, axis=0)
        out_sorted = expert_ffn(sorted_rows, group_sizes, w_one, w_three, w_two)
        out_rows = jnp.take(out_sorted, jnp.argsort(sort_order), axis=0)
        back_rows = lax.all_to_all(out_rows.reshape(dev_count, row_cap, model_dim), "ep", 0, 0, tiled=True)
        picked_rows = jnp.take(back_rows.reshape(dev_count * row_cap, model_dim), slot_pos, axis=0)
        both_out = picked_rows.reshape(tok_count, 2, model_dim).astype(jnp.float32)
        return jnp.sum(gate_vals[:, :, None] * both_out, axis=1).astype(jnp.bfloat16)

    return jax.shard_map(device_body, mesh=mesh, in_specs=(P("ep", None), P(None, None), P("ep", None), P("ep", None, None), P("ep", None, None), P("ep", None, None)), out_specs=P("ep", None), check_vma=False)
```

profile of v0, /device:TPU:0, one launch (start us, length us, event | category | flops | bytes accessed | tf_op | source)
XLA Modules:
  0.0 197.1 jit_solution(2077754783558539928)
XLA Ops:
  0.0 0.8 copy.37
  1.1 0.7 broadcast_multiply_fusion
  1.8 0.6 reduce-window.6
  3.0 1.4 scatter_custom_fusion.1
  4.4 0.7 all_to_all.13
  5.1 4.3 %all-to-all-start.1 = ((s32[8,1,64]{2,1,0:T(1,128)}), s32[8,1,64]{2,1,0:T(1,128)S(1)}, u32[]{:S(2)}, u32[]{:S(2)}) async-start(s32[8,1,64]{2,1,0:T(1,128)} %all_to_all.13), calls=%async_computation.1 | async-start | bytes 8192 | tf_op jit(solution)/shard_map/all_to_all | solution.py:40
  9.4 1.4 scatter_custom_fusion
  10.9 2.5 %gather_fusion = bf16[512,2048]{1,0:T(8,128)(2,1)S(1)} fusion(bf16[128,2048]{1,0:T(8,128)(2,1)S(1)} %copy-done, s32[1024]{0:T(1024)S(1)} %pad_clamp_fusion.3), kind=kCustom, calls=%fused_computation.2 | custom fusion | bytes 4196352 | tf_op jit(solution)/shard_map/jit(_take)/gather | solution.py:38
  13.4 1.6 broadcast_select_fusion.2
  15.0 2.9 %all-to-all-start = ((bf16[8,64,2048]{2,1,0:T(8,128)(2,1)}), bf16[8,64,2048]{2,1,0:T(8,128)(2,1)S(1)}, u32[]{:S(2)}, u32[]{:S(2)}) async-start(bf16[8,64,2048]{2,1,0:T(8,128)(2,1)} %broadcast_select_fusion.2), calls=%async_computation | async-start | bytes 4194304 | tf_op jit(solution)/shard_map/all_to_all | solution.py:39
  17.9 0.5 broadcast.206
  18.5 0.7 reduce.7
  19.2 0.6 convert_reduce_fusion
  19.8 1.2 ragged-dot-metadata
  21.1 3.8 %sort.34 = (s32[512]{0:T(512)}, s32[512]{0:T(512)S(1)}) sort(s32[512]{0:T(512)S(1)} %reshape.136, s32[512]{0:T(512)S(1)} %iota.20), dimensions={0}, to_apply=%region_8.9 | sort | flops 4608 | bytes 8192 | tf_op jit(solution)/shard_map/jit(argsort)/sort | solution.py:42
  24.8 3.8 %sort.35 = (s32[512]{0:T(512)}, s32[512]{0:T(512)S(1)}) sort(s32[512]{0:T(512)S(1)} %get-tuple-element.8, s32[512]{0:T(512)S(1)} %iota.21), dimensions={0}, to_apply=%region_10.12 | sort | flops 4608 | bytes 8192 | tf_op jit(solution)/shard_map/jit(argsort)/sort | solution.py:46
  28.7 15.9 %all-to-all-done = bf16[8,64,2048]{2,1,0:T(8,128)(2,1)S(1)} async-done(((bf16[8,64,2048]{2,1,0:T(8,128)(2,1)}), bf16[8,64,2048]{2,1,0:T(8,128)(2,1)S(1)}, u32[]{:S(2)}, u32[]{:S(2)}) %all-to-all-start) | async-done | bytes 2097184 | tf_op jit(solution)/shard_map/all_to_all | solution.py:39
  44.5 3.3 %gather_fusion.3 = bf16[512,2048]{1,0:T(8,128)(2,1)} fusion(bf16[512,2048]{1,0:T(8,128)(2,1)S(1)} %bitcast.20, s32[1024]{0:T(1024)S(1)} %pad_clamp_fusion.2), kind=kCustom, calls=%fused_computation.clone | custom fusion | bytes 4196352 | tf_op jit(solution)/shard_map/jit(_take)/gather | solution.py:44
  47.8 3.2 %broadcast_select_fusion.1 = bf16[512,2048]{1,0:T(8,128)(2,1)} fusion(bf16[512,2048]{1,0:T(8,128)(2,1)} %gather_fusion.3, pred[512]{0:T(512)(128)(4,1)S(1)} %compare_and_fusion.1), kind=kLoop, calls=%fused_computation.10 | loop fusion | flops 1048576 | bytes 4194816 | tf_op jit(solution)/shard_map/jit(_take)/select_n | solution.py:44
  51.0 27.6 %ragged-dot-none.2 = f32[512,5632]{1,0:T(8,128)} custom-call(s32[1]{0:T(128)} %get-tuple-element.10, s32[2]{0:T(128)} %get-tuple-element.11, s32[2]{0:T(128)} %get-tuple-element.12, s32[2]{0:T(128)} %get-tuple-element.13, s32[1]{0:T(128)} %get-tuple-element.10, bf16[512,2048]{1,0:T(8,128)(2,1)} %broadcast_select_fusion.1, bf16[1,2048,5632]{2,1,0:T(8,128)(2,1)} %param.11), custom_call_target="tpu_custom_call" | custom-call | flops 11811160064 | bytes 36700164 | tf_op jit(solution)/shard_map/ragged_dot_general/ragged-dot-none
  78.6 27.8 %ragged-dot-none.1 = f32[512,5632]{1,0:T(8,128)} custom-call(s32[1]{0:T(128)} %get-tuple-element.10, s32[2]{0:T(128)} %get-tuple-element.11, s32[2]{0:T(128)} %get-tuple-element.12, s32[2]{0:T(128)} %get-tuple-element.13, s32[1]{0:T(128)} %get-tuple-element.10, bf16[512,2048]{1,0:T(8,128)(2,1)} %broadcast_select_fusion.1, bf16[1,2048,5632]{2,1,0:T(8,128)(2,1)} %param.12), custom_call_target="tpu_custom_call" | custom-call | flops 11811160064 | bytes 36700164 | tf_op jit(solution)/shard_map/ragged_dot_general/ragged-dot-none
  106.4 11.6 %multiply_convert_fusion = bf16[512,5632]{1,0:T(8,128)(2,1)} fusion(f32[512,5632]{1,0:T(8,128)} %ragged-dot-none.1, f32[512,5632]{1,0:T(8,128)} %ragged-dot-none.2), kind=kLoop, calls=%fused_computation.7 | loop fusion | flops 17301504 | bytes 28835840 | tf_op jit(solution)/shard_map/convert_element_type | solution.py:17
  118.0 32.0 %ragged-dot-none = f32[512,2048]{1,0:T(8,128)} custom-call(s32[1]{0:T(128)} %get-tuple-element.10, s32[2]{0:T(128)} %get-tuple-element.11, s32[2]{0:T(128)} %get-tuple-element.12, s32[2]{0:T(128)} %get-tuple-element.13, s32[1]{0:T(128)} %get-tuple-element.10, bf16[512,5632]{1,0:T(8,128)(2,1)} %multiply_convert_fusion, bf16[1,5632,2048]{2,1,0:T(8,128)(2,1)} %param.13), custom_call_target="tpu_custom_call" | custom-call | flops 11811160064 | bytes 33030148 | tf_op jit(solution)/shard_map/ragged_dot_general/ragged-dot-none
  150.0 2.5 %convert_element_type.28 = bf16[512,2048]{1,0:T(8,128)(2,1)S(1)} convert(f32[512,2048]{1,0:T(8,128)} %ragged-dot-none) | non-fusion elementwise | flops 1048576 | bytes 6291456 | tf_op jit(solution)/shard_map/convert_element_type | solution.py:18
  152.6 3.3 %gather_fusion.4 = bf16[512,2048]{1,0:T(8,128)(2,1)} fusion(bf16[512,2048]{1,0:T(8,128)(2,1)S(1)} %convert_element_type.28, s32[1024]{0:T(1024)S(1)} %pad_clamp_fusion.1), kind=kCustom, calls=%fused_computation.1.clone | custom fusion | bytes 4196352 | tf_op jit(solution)/shard_map/jit(_take)/gather | solution.py:46
  155.9 3.2 %broadcast_select_fusion = bf16[512,2048]{1,0:T(8,128)(2,1)} fusion(bf16[512,2048]{1,0:T(8,128)(2,1)} %gather_fusion.4, pred[512]{0:T(512)(128)(4,1)S(1)} %compare_and_fusion), kind=kLoop, calls=%fused_computation.9 | loop fusion | flops 1048576 | bytes 4194816 | tf_op jit(solution)/shard_map/jit(_take)/select_n | solution.py:46
  159.1 2.7 %all-to-all-start.2 = ((bf16[8,64,2048]{2,1,0:T(8,128)(2,1)}), bf16[8,64,2048]{2,1,0:T(8,128)(2,1)S(1)}, u32[]{:S(2)}, u32[]{:S(2)}) async-start(bf16[8,64,2048]{2,1,0:T(8,128)(2,1)} %bitcast.23), calls=%async_computation.2 | async-start | bytes 4194304 | tf_op jit(solution)/shard_map/all_to_all | solution.py:47
  162.5 1.4 gather_fusion.2
  164.5 23.6 %all-to-all-done.2 = bf16[8,64,2048]{2,1,0:T(8,128)(2,1)S(1)} async-done(((bf16[8,64,2048]{2,1,0:T(8,128)(2,1)}), bf16[8,64,2048]{2,1,0:T(8,128)(2,1)S(1)}, u32[]{:S(2)}, u32[]{:S(2)}) %all-to-all-start.2) | async-done | bytes 2097184 | tf_op jit(solution)/shard_map/all_to_all | solution.py:47
  188.1 2.3 %gather_fusion.1 = bf16[256,2048]{1,0:T(8,128)(2,1)} fusion(bf16[512,2048]{1,0:T(8,128)(2,1)S(1)} %bitcast.21, s32[1024]{0:T(1024)S(1)} %pad_clamp_fusion), kind=kCustom, calls=%fused_computation.3 | custom fusion | bytes 2098176 | tf_op jit(solution)/shard_map/jit(_take)/gather | solution.py:48
  190.5 1.7 gather.23
  192.2 4.9 %multiply_reduce_fusion = bf16[128,2048]{1,0:T(8,128)(2,1)} fusion(bf16[128,2,2048]{2,1,0:T(2,128)(2,1)S(1)} %gather.23, pred[128,2]{1,0:T(8,128)(4,1)S(1)} %copy.40, f32[128,2]{1,0:T(8,128)S(1)} %copy.36), kind=kLoop, calls=%fused_computation.8 | loop fusion | flops 1835008 | bytes 1574144 | tf_op jit(solution)/shard_map/reduce_sum | solution.py:50
  (49 shorter events, 2.4 us)
Async XLA Ops:
  0.0 10.9 %copy-start = (bf16[128,2048]{1,0:T(8,128)(2,1)S(1)}, bf16[128,2048]{1,0:T(8,128)(2,1)}, u32[]{:S(2)}) copy-start(bf16[128,2048]{1,0:T(8,128)(2,1)} %param.8) | copy-start | bytes 1572868
  5.1 9.9 %all-to-all-start.1 = ((s32[8,1,64]{2,1,0:T(1,128)}), s32[8,1,64]{2,1,0:T(1,128)S(1)}, u32[]{:S(2)}, u32[]{:S(2)}) async-start(s32[8,1,64]{2,1,0:T(1,128)} %all_to_all.13), calls=%async_computation.1 | async-start | bytes 8192 | tf_op jit(solution)/shard_map/all_to_all | solution.py:40
  15.0 29.5 %all-to-all-start = ((bf16[8,64,2048]{2,1,0:T(8,128)(2,1)}), bf16[8,64,2048]{2,1,0:T(8,128)(2,1)S(1)}, u32[]{:S(2)}, u32[]{:S(2)}) async-start(bf16[8,64,2048]{2,1,0:T(8,128)(2,1)} %broadcast_select_fusion.2), calls=%async_computation | async-start | bytes 4194304 | tf_op jit(solution)/shard_map/all_to_all | solution.py:39
  159.1 2.8 %copy-start.2 = (s32[128,2]{0,1:T(2,128)S(1)}, s32[128,2]{0,1:T(2,128)}, u32[]{:S(2)}) copy-start(s32[128,2]{0,1:T(2,128)} %param.10) | copy-start | bytes 3076
  159.1 3.1 %copy-start.1 = (f32[2048,8]{0,1:T(8,128)S(1)}, f32[2048,8]{0,1:T(8,128)}, u32[]{:S(2)}) copy-start(f32[2048,8]{0,1:T(8,128)} %param.9) | copy-start | bytes 196612
  159.1 29.0 %all-to-all-start.2 = ((bf16[8,64,2048]{2,1,0:T(8,128)(2,1)}), bf16[8,64,2048]{2,1,0:T(8,128)(2,1)S(1)}, u32[]{:S(2)}, u32[]{:S(2)}) async-start(bf16[8,64,2048]{2,1,0:T(8,128)(2,1)} %bitcast.23), calls=%async_computation.2 | async-start | bytes 4194304 | tf_op jit(solution)/shard_map/all_to_all | solution.py:47
where the time goes:
time: 196 us; the launch traced here: 197 us
  Pallas kernels  88.6 us (45%)
  waiting for transfers between devices  39.4 us (20%)
  other arithmetic  37.4 us (19%)
  local copies, waits for them, and re-layouts  21.2 us (11%)
  starting transfers between devices  9.92 us (5%)
    another operation x3, Pallas kernels  87.4 us
    all_to_all x1, waiting for transfers between devices, device_body(): lax.all_to_all(out_rows.reshape(dev_count, row_cap, model_dim), 'ep', 0,...  23.6 us
    all_to_all x1, waiting for transfers between devices, device_body(): recv_rows = lax.all_to_all(send_rows, 'ep', 0, 0, tiled=True)  15.9 us
    convert_element_type x1, other arithmetic, expert_ffn(): act_rows = (jax.nn.silu(h_one) * h_three).astype(jnp.bfloat16)  11.6 us
    reduce_sum x1, other arithmetic, device_body(): jnp.sum(gate_vals[:, :, None] * both_out, axis=1).astype(jnp.bfloat16)  4.92 us
    all_to_all x1, starting transfers between devices, device_body(): lax.all_to_all(send_exp.reshape(dev_count, row_cap), 'ep', 0, 0, tiled=True)  4.3 us
    gather x2, local copies, waits for them, and re-layouts, device_body(): jnp.take(back_rows.reshape(dev_count * row_cap, model_dim), slot_pos, axi...  4.09 us
  transfers between devices with their start and end apart: 3, of which 2 were waited for; matrix products, arithmetic and copies ran while one was open for 9% of the time, Pallas kernels for 1%

commit v1 on v0

v1 whole, which is shorter than its diff:
```python
import functools

import jax
import jax.numpy as jnp
from jax import lax
from jax.experimental import pallas as pl
from jax.experimental.pallas import tpu as pltpu
from jax.sharding import PartitionSpec as P

MESH = pl.DeviceIdType.MESH
N_DEV = 8
CAP = 64
TOK = 128
TN = 512
SPLIT = 6
ROW_ORDER = (6, 7, 0, 1, 2, 4, 3, 5)
POS = tuple(ROW_ORDER.index(k) for k in range(N_DEV))
F32 = jnp.float32
BF16 = jnp.bfloat16


def peer_of(me, k):
    for bit in (1, 2, 4):
        if k & bit:
            me = me + bit - 2 * bit * ((me // bit) % 2)
    return me


def dot(a, b):
    return jnp.dot(a, b, preferred_element_type=F32)


def moe_kernel(hid_hbm, router_hbm, ids_hbm, w1_hbm, w3_hbm, w2_hbm, out_hbm,
               hid, router, ids, x, xsend, back, h, pool, keyt,
               in_sem, pool_sem, xs_sem, xr_sem, rs_sem, rr_sem, out_sem):
    me = lax.axis_index("ep")
    d_model = hid.shape[1]
    ff = h.shape[1]
    n_ff = ff // TN
    n_out = d_model // TN
    kparts = [(s, min(d_model, ff - s)) for s in range(0, ff, d_model)]
    n_k = len(kparts)
    w2_home = 2 * n_ff

    ids_copy = pltpu.make_async_copy(ids_hbm, ids, in_sem.at[0])
    hid_copy = pltpu.make_async_copy(hid_hbm, hid, in_sem.at[1])
    router_copy = pltpu.make_async_copy(router_hbm, router, in_sem.at[2])
    ids_copy.start()
    hid_copy.start()

    def up_copies(j):
        cols = pl.ds(pl.multiple_of(j * TN, TN), TN)
        return (pltpu.make_async_copy(w1_hbm.at[0, :, cols], pool.at[2 * j], pool_sem.at[2 * j]),
                pltpu.make_async_copy(w3_hbm.at[0, :, cols], pool.at[2 * j + 1], pool_sem.at[2 * j + 1]))

    def down_copies(n, base):
        cols = pl.ds(pl.multiple_of(n * TN, TN), TN)
        return [pltpu.make_async_copy(w2_hbm.at[0, pl.ds(s, size), cols], pool.at[base + i, pl.ds(0, size), :],
                                      pool_sem.at[base + i]) for i, (s, size) in enumerate(kparts)]

    def start_all(copies):
        for c in copies:
            c.start()

    def wait_all(copies):
        for c in copies:
            c.wait()

    @pl.loop(0, n_ff)
    def _(j):
        start_all(up_copies(j))

    router_copy.start()
    start_all(down_copies(0, w2_home))

    barrier = pltpu.get_barrier_semaphore()
    for k in range(1, N_DEV):
        pl.semaphore_signal(barrier, inc=1, device_id=(peer_of(me, k),), device_id_type=MESH)

    ids_copy.wait()
    lane = lax.broadcasted_iota(jnp.int32, (TOK, TOK), 1)
    row = lax.broadcasted_iota(jnp.int32, (TOK, TOK), 0)
    expert = lax.broadcasted_iota(jnp.int32, (N_DEV, TOK), 0)
    chosen = jnp.where((expert == ids[0:1, :]) | (expert == ids[1:2, :]), 1.0, 0.0)
    before = jnp.where(row < lane, 1.0, 0.0)
    rank = dot(chosen.astype(BF16), before.astype(BF16))
    keyt[...] = jnp.where(chosen > 0.0, rank, -1.0)
    slot = lax.broadcasted_iota(jnp.int32, (CAP, TOK), 0).astype(F32)

    def select(k):
        return jnp.where(slot == keyt[pl.ds(peer_of(me, k), 1), :], 1.0, 0.0).astype(BF16)

    def send_copy(k):
        return pltpu.make_async_remote_copy(
            src_ref=xsend.at[pl.ds((k - 1) * CAP, CAP), :], dst_ref=x.at[pl.ds(POS[k] * CAP, CAP), :],
            send_sem=xs_sem.at[k], recv_sem=xr_sem.at[k], device_id=(peer_of(me, k),), device_id_type=MESH)

    hid_copy.wait()

    def pack(ks):
        pick = jnp.concatenate([select(k) for k in ks], axis=0)
        for n in range(n_out):
            cols = pl.ds(n * TN, TN)
            rows = dot(pick, hid[:, cols]).astype(BF16)
            for i, k in enumerate(ks):
                piece = rows[i * CAP:(i + 1) * CAP]
                if k == 0:
                    x[pl.ds(POS[0] * CAP, CAP), cols] = piece
                else:
                    xsend[pl.ds((k - 1) * CAP, CAP), cols] = piece

    pack((2, 4, 1, 0))
    pl.semaphore_wait(barrier, N_DEV - 1)
    for k in (2, 4, 1):
        send_copy(k).start()
    pack((3, 5, 6, 7))
    for k in (3, 5, 6, 7):
        send_copy(k).start()

    own, near, late, far = 128, 256, 384, 0

    def h_row(r):
        return far if r == late else r

    def up_tile(j, r0, rows):
        xr = x[pl.ds(r0, rows), :]
        half = TN // 2
        for c in range(2):
            cols = pl.ds(c * half, half)
            u = dot(xr, pool[2 * j, :, cols])
            v = dot(xr, pool[2 * j + 1, :, cols])
            act = (jax.nn.silu(u) * v).astype(BF16)
            cols = pl.ds(pl.multiple_of(j * TN + c * half, half), half)
            for i in range(0, rows, 128):
                h[pl.ds(h_row(r0 + i), 128), cols] = act[i:i + 128]

    def return_copy(k, n):
        cols = pl.ds(pl.multiple_of(n * TN, TN), TN)
        return pltpu.make_async_remote_copy(
            src_ref=x.at[pl.ds(POS[k] * CAP, CAP), cols], dst_ref=back.at[pl.ds(k * CAP, CAP), cols],
            send_sem=rs_sem.at[k, n], recv_sem=rr_sem.at[k, n], device_id=(peer_of(me, k),), device_id_type=MESH)

    def down_tile(n, base, r0, rows):
        cols = pl.ds(pl.multiple_of(n * TN, TN), TN)
        acc = None
        for i, (s, size) in enumerate(kparts):
            act = jnp.concatenate([h[pl.ds(h_row(r0 + m), 128), pl.ds(s, size)] for m in range(0, rows, 128)], axis=0)
            part = dot(act, pool[base + i, pl.ds(0, size), :])
            acc = part if acc is None else acc + part
        res = acc.astype(BF16)
        x[pl.ds(r0, rows), cols] = res
        for i in range(rows // CAP):
            k = ROW_ORDER[r0 // CAP + i]
            if k == 0:
                back[pl.ds(0, CAP), cols] = res[i * CAP:(i + 1) * CAP]
            else:
                return_copy(k, n).start()

    send_copy(1).wait_recv()

    @pl.loop(0, SPLIT)
    def _(j):
        wait_all(up_copies(j))
        up_tile(j, own, 128)

    send_copy(2).wait_recv()
    send_copy(4).wait_recv()

    @pl.loop(SPLIT, n_ff)
    def _(j):
        wait_all(up_copies(j))
        up_tile(j, own, 256)

    send_copy(3).wait_recv()
    send_copy(5).wait_recv()

    @pl.loop(0, SPLIT)
    def _(j):
        up_tile(j, near, 256)

    @pl.loop(SPLIT, n_ff)
    def _(j):
        up_tile(j, late, 128)

    start_all(down_copies(1, w2_home - n_k))
    start_all(down_copies(2, w2_home - 2 * n_k))

    @pl.loop(0, n_out)
    def _(n):
        base = w2_home - n_k * (n % 3)
        wait_all(down_copies(n, base))
        down_tile(n, base, near, 256)

        @pl.when(n == 0)
        def _():
            start_all(down_copies(3, w2_home))

    kept = (w2_home - 2 * n_k) // 2

    @pl.loop(kept, n_ff)
    def _(j):
        start_all(up_copies(j))

    start_all(down_copies(0, w2_home))
    send_copy(6).wait_recv()
    send_copy(7).wait_recv()

    @pl.loop(0, kept)
    def _(j):
        up_tile(j, far, 128)

    n_slots = w2_home + n_k
    for n in range(1, n_out):
        start_all(down_copies(n, (w2_home + n_k * n) % n_slots))

    @pl.loop(kept, n_ff)
    def _(j):
        wait_all(up_copies(j))
        up_tile(j, far, 128)

    @pl.loop(0, n_out)
    def _(n):
        base = (w2_home + n_k * n) % n_slots
        wait_all(down_copies(n, base))
        down_tile(n, base, far, 256)

    router_copy.wait()
    w = router[...]
    w_hi = w.astype(BF16)
    rest = w - w_hi.astype(F32)
    w_mid = rest.astype(BF16)
    w_lo = (rest - w_mid.astype(F32)).astype(BF16)
    xh = hid[...]

    def logit_part(piece):
        return lax.dot_general(piece, xh, (((1,), (1,)), ((), ())), preferred_element_type=F32)

    logits = (logit_part(w_lo) + logit_part(w_mid)) + logit_part(w_hi)
    ex = jnp.exp(logits - jnp.max(logits, axis=0, keepdims=True))
    prob = ex / jnp.sum(ex, axis=0, keepdims=True)
    gates, wheres = [], []
    for c in range(2):
        hit = expert == ids[c:c + 1, :]
        gates.append(jnp.sum(jnp.where(hit, prob, 0.0), axis=0, keepdims=True))
        r = jnp.sum(jnp.where(hit, keyt[...], 0.0), axis=0, keepdims=True)
        wheres.append((ids[c:c + 1, :] ^ me).astype(F32) * float(CAP) + r)
    total = gates[0] + gates[1]
    cols4 = jnp.concatenate([gates[0] / total, gates[1] / total, wheres[0], wheres[1]]
                            + [jnp.zeros((TOK - 4, TOK), F32)], axis=0).T
    g0, g1 = cols4[:, 0:1], cols4[:, 1:2]

    wide = lax.broadcasted_iota(jnp.int32, (TOK, N_DEV * CAP), 1).astype(F32)
    pick = jnp.concatenate([jnp.where(wide == cols4[:, 2 + c:3 + c], 1.0, 0.0).astype(BF16) for c in range(2)],
                           axis=0)

    out_copies = []
    for n in range(n_out):
        cols = pl.ds(n * TN, TN)
        for k in range(1, N_DEV):
            return_copy(k, n).wait_recv()
        both = dot(pick, back[:, cols])
        hid[:, cols] = (g0 * both[:TOK] + g1 * both[TOK:]).astype(BF16)
        c = pltpu.make_async_copy(hid.at[:, cols], out_hbm.at[:, cols], out_sem.at[n])
        c.start()
        out_copies.append(c)
    for k in range(1, N_DEV):
        send_copy(k).wait_send()
        for n in range(n_out):
            return_copy(k, n).wait_send()
    wait_all(out_copies)


def solution(mesh):
    def device_body(hidden, w_router, ids, w_one, w_three, w_two):
        d_model, ff = w_one.shape[1:]
        n_exp = w_router.shape[1]
        rows = N_DEV * CAP
        n_out = d_model // TN
        n_slots = 2 * (ff // TN) + -(-ff // d_model)
        dma = pltpu.SemaphoreType.DMA
        return pl.pallas_call(
            moe_kernel,
            out_shape=jax.ShapeDtypeStruct(hidden.shape, BF16),
            in_specs=[pl.BlockSpec(memory_space=pl.ANY)] * 6,
            out_specs=pl.BlockSpec(memory_space=pl.ANY),
            scratch_shapes=[
                pltpu.VMEM((TOK, d_model), BF16),
                pltpu.VMEM((n_exp, d_model), F32),
                pltpu.VMEM((2, TOK), jnp.int32),
                pltpu.VMEM((rows, d_model), BF16),
                pltpu.VMEM((rows - CAP, d_model), BF16),
                pltpu.VMEM((rows, d_model), BF16),
                pltpu.VMEM((rows - 128, ff), BF16),
                pltpu.VMEM((n_slots, d_model, TN), BF16),
                pltpu.VMEM((n_exp, TOK), F32),
                dma((3,)), dma((n_slots,)), dma((N_DEV,)), dma((N_DEV,)),
                dma((N_DEV, n_out)), dma((N_DEV, n_out)), dma((n_out,)),
            ],
            compiler_params=pltpu.CompilerParams(
                collective_id=0, has_side_effects=True, vmem_limit_bytes=67043328),
        )(hidden, w_router.T, ids.T, w_one, w_three, w_two)

    return jax.shard_map(
        device_body, mesh=mesh,
        in_specs=(P("ep", None), P(None, None), P("ep", None), P("ep", None, None), P("ep", None, None), P("ep", None, None)),
        out_specs=P("ep", None), check_vma=False)
```

time: 196 us -> 67.6 us (0.34)
  the two profiles are of different devices: /device:TPU:0 before, /device:TPU:2 now
where the time goes in v1:
time: 67.6 us; the launch traced here: 67.5 us
  Pallas kernels  65.6 us (97%)
  local copies, waits for them, and re-layouts  1.88 us (3%)
    pallas_call x1, Pallas kernels, device_body(): pl.pallas_call(moe_kernel, out_shape=jax.ShapeDtypeStruct(hidden.shape, B...  65.6 us
    unnamed x1, local copies, waits for them, and re-layouts  1.88 us

profile of v1, /device:TPU:2, one launch (start us, length us, event | category | flops | bytes accessed | tf_op | source)
XLA Modules:
  0.0 67.5 jit_solution(14121751998132065608)
XLA Ops:
  0.0 65.6 %shard_map.64 = bf16[128,2048]{1,0:T(8,128)(2,1)} custom-call(bf16[128,2048]{1,0:T(8,128)(2,1)} %hid_hbm.1, f32[8,2048]{1,0:T(8,128)} %bitcast.2, s32[2,128]{1,0:T(2,128)} %bitcast.3, bf16[1,2048,5632]{2,1,0:T(8,128)(2,1)} %w1_hbm.1, bf16[1,2048,5632]{2,1,0:T(8,128)(2,1)} %w3_hbm.1, bf16[1,5632,2048]{2,1,0:T(8,128)(2,1)} %w2_hbm.1), custom_call_target="tpu_custom_call" | custom-call | tf_op jit(solution)/shard_map/pallas_call | solution.py:281
  65.6 1.9 %copy.8 = bf16[128,2048]{1,0:T(8,128)(2,1)} copy(bf16[128,2048]{1,0:T(8,128)(2,1)} %shard_map.64) | data formatting | bytes 1048576

commit v2 on v1

--- a/solution.py
+++ b/solution.py
@@ -114,7 +114,7 @@
     for k in (2, 4, 1):
         send_copy(k).start()
     pack((3, 5, 6, 7))
-    for k in (3, 5, 6, 7):
+    for k in (3, 5):
         send_copy(k).start()
 
     own, near, late, far = 128, 256, 384, 0
@@ -171,6 +171,8 @@
         wait_all(up_copies(j))
         up_tile(j, own, 256)
 
+    for k in (6, 7):
+        send_copy(k).start()
     send_copy(3).wait_recv()
     send_copy(5).wait_recv()
 

time: 67.6 us -> 64.5 us (0.954)
  the two profiles are of different devices: /device:TPU:2 before, /device:TPU:0 now
where the time goes in v2:
time: 64.5 us; the launch traced here: 64.4 us
  Pallas kernels  62.5 us (97%)
  local copies, waits for them, and re-layouts  1.88 us (3%)
    pallas_call x1, Pallas kernels, device_body(): pl.pallas_call(moe_kernel, out_shape=jax.ShapeDtypeStruct(hidden.shape, B...  62.5 us
    unnamed x1, local copies, waits for them, and re-layouts  1.88 us

profile of v2, /device:TPU:0, one launch (start us, length us, event | category | flops | bytes accessed | tf_op | source)
XLA Modules:
  0.0 64.4 jit_solution(1910151540418428411)
XLA Ops:
  0.0 62.5 %shard_map.64 = bf16[128,2048]{1,0:T(8,128)(2,1)} custom-call(bf16[128,2048]{1,0:T(8,128)(2,1)} %hid_hbm.1, f32[8,2048]{1,0:T(8,128)} %bitcast.2, s32[2,128]{1,0:T(2,128)} %bitcast.3, bf16[1,2048,5632]{2,1,0:T(8,128)(2,1)} %w1_hbm.1, bf16[1,2048,5632]{2,1,0:T(8,128)(2,1)} %w3_hbm.1, bf16[1,5632,2048]{2,1,0:T(8,128)(2,1)} %w2_hbm.1), custom_call_target="tpu_custom_call" | custom-call | tf_op jit(solution)/shard_map/pallas_call | solution.py:283
  62.5 1.9 %copy.8 = bf16[128,2048]{1,0:T(8,128)(2,1)} copy(bf16[128,2048]{1,0:T(8,128)(2,1)} %shard_map.64) | data formatting | bytes 1048576

commit v3 on v2

--- a/solution.py
+++ b/solution.py
@@ -114,117 +114,143 @@
     for k in (2, 4, 1):
         send_copy(k).start()
     pack((3, 5, 6, 7))
-    for k in (3, 5):
-        send_copy(k).start()
-
-    own, near, late, far = 128, 256, 384, 0
-
-    def h_row(r):
-        return far if r == late else r
-
-    def up_tile(j, r0, rows):
+
+    group = 128
+    far, own, near, late = 0, group, 2 * group, 3 * group
+
+    def up_tile(j, r0, h0, rows):
         xr = x[pl.ds(r0, rows), :]
         half = TN // 2
         for c in range(2):
             cols = pl.ds(c * half, half)
             u = dot(xr, pool[2 * j, :, cols])
             v = dot(xr, pool[2 * j + 1, :, cols])
-            act = (jax.nn.silu(u) * v).astype(BF16)
-            cols = pl.ds(pl.multiple_of(j * TN + c * half, half), half)
-            for i in range(0, rows, 128):
-                h[pl.ds(h_row(r0 + i), 128), cols] = act[i:i + 128]
+            h[pl.ds(h0, rows), pl.ds(pl.multiple_of(j * TN + c * half, half), half)] = (
+                jax.nn.silu(u) * v).astype(BF16)
 
     def return_copy(k, n):
-        cols = pl.ds(pl.multiple_of(n * TN, TN), TN)
+        cols = pl.ds(n * TN, TN)
         return pltpu.make_async_remote_copy(
             src_ref=x.at[pl.ds(POS[k] * CAP, CAP), cols], dst_ref=back.at[pl.ds(k * CAP, CAP), cols],
             send_sem=rs_sem.at[k, n], recv_sem=rr_sem.at[k, n], device_id=(peer_of(me, k),), device_id_type=MESH)
 
-    def down_tile(n, base, r0, rows):
-        cols = pl.ds(pl.multiple_of(n * TN, TN), TN)
+    def down_tile(n, base, r0, h0):
+        cols = pl.ds(n * TN, TN)
         acc = None
         for i, (s, size) in enumerate(kparts):
-            act = jnp.concatenate([h[pl.ds(h_row(r0 + m), 128), pl.ds(s, size)] for m in range(0, rows, 128)], axis=0)
-            part = dot(act, pool[base + i, pl.ds(0, size), :])
+            part = dot(h[pl.ds(h0, group), pl.ds(s, size)], pool[base + i, pl.ds(0, size), :])
             acc = part if acc is None else acc + part
         res = acc.astype(BF16)
-        x[pl.ds(r0, rows), cols] = res
-        for i in range(rows // CAP):
+        x[pl.ds(r0, group), cols] = res
+        for i in range(group // CAP):
             k = ROW_ORDER[r0 // CAP + i]
             if k == 0:
                 back[pl.ds(0, CAP), cols] = res[i * CAP:(i + 1) * CAP]
-            else:
+
+    def give_back(n, r0):
+        for i in range(group // CAP):
+            k = ROW_ORDER[r0 // CAP + i]
+            if k:
                 return_copy(k, n).start()
 
     send_copy(1).wait_recv()
 
-    @pl.loop(0, SPLIT)
+    @pl.loop(0, SPLIT - 1)
     def _(j):
         wait_all(up_copies(j))
-        up_tile(j, own, 128)
-
+        up_tile(j, own, 0, group)
+
+    for k in (2, 4):
+        send_copy(k).wait_send()
+    for k in (6, 7):
+        send_copy(k).start()
+    wait_all(up_copies(SPLIT - 1))
+    up_tile(SPLIT - 1, own, 0, group)
     send_copy(2).wait_recv()
     send_copy(4).wait_recv()
 
     @pl.loop(SPLIT, n_ff)
     def _(j):
         wait_all(up_copies(j))
-        up_tile(j, own, 256)
-
-    for k in (6, 7):
+        up_tile(j, own, 0, 2 * group)
+
+    q1, q2 = w2_home - n_k, w2_home - 2 * n_k
+    start_all(down_copies(1, q1))
+    start_all(down_copies(2, q2))
+
+    @pl.loop(0, SPLIT, step=3)
+    def _(j):
+        for i in range(3):
+            up_tile(j + i, near, group, group)
+
+    for k in (3, 5):
         send_copy(k).start()
+
+    def up_slot(s):
+        cols = pl.ds((s // 2) * TN, TN)
+        return pltpu.make_async_copy((w3_hbm if s % 2 else w1_hbm).at[0, :, cols], pool.at[s], pool_sem.at[s])
+
+    def down_pass(steps, r0):
+        for n, base, after in steps:
+            wait_all(down_copies(n, base))
+            down_tile(n, base, r0, group)
+            start_all(after)
+            give_back(n, r0)
+
+    down_pass([(0, w2_home, down_copies(3, w2_home)),
+               (1, q1, [up_slot(s) for s in range(q1, q1 + n_k)]),
+               (2, q2, [up_slot(s) for s in range(q2, q2 + n_k)]),
+               (3, w2_home, [])], near)
+
+    send_copy(6).wait_recv()
+    send_copy(7).wait_recv()
+
+    @pl.loop(0, 8, step=4)
+    def _(j):
+        for i in range(4):
+            up_tile(j + i, far, group, group)
+
+        @pl.when(j == 0)
+        def _():
+            start_all(down_copies(1, 0))
+            start_all(down_copies(2, n_k))
+
+    wait_all([up_slot(s) for s in range(q2, w2_home)])
+    for j in range(8, n_ff):
+        up_tile(j, far, group, group)
+    down_tile(3, w2_home, far, group)
+    start_all(down_copies(0, w2_home))
+    give_back(3, far)
+    down_pass([(1, 0, [up_slot(s) for s in range(0, n_k)]),
+               (2, n_k, [up_slot(s) for s in range(n_k, 2 * n_k)]),
+               (0, w2_home, [])], far)
+
     send_copy(3).wait_recv()
     send_copy(5).wait_recv()
-
-    @pl.loop(0, SPLIT)
-    def _(j):
-        up_tile(j, near, 256)
-
-    @pl.loop(SPLIT, n_ff)
-    def _(j):
-        up_tile(j, late, 128)
-
-    start_all(down_copies(1, w2_home - n_k))
-    start_all(down_copies(2, w2_home - 2 * n_k))
-
-    @pl.loop(0, n_out)
-    def _(n):
-        base = w2_home - n_k * (n % 3)
-        wait_all(down_copies(n, base))
-        down_tile(n, base, near, 256)
-
-        @pl.when(n == 0)
+    c1, c2, c3 = 2 * n_k, 3 * n_k, 4 * n_k
+
+    @pl.loop(3, n_ff, step=4)
+    def _(j):
+        for i in range(4):
+            up_tile(j + i, late, group, group)
+
+        @pl.when(j == 3)
         def _():
-            start_all(down_copies(3, w2_home))
-
-    kept = (w2_home - 2 * n_k) // 2
-
-    @pl.loop(kept, n_ff)
-    def _(j):
-        start_all(up_copies(j))
-
-    start_all(down_copies(0, w2_home))
-    send_copy(6).wait_recv()
-    send_copy(7).wait_recv()
-
-    @pl.loop(0, kept)
-    def _(j):
-        up_tile(j, far, 128)
-
-    n_slots = w2_home + n_k
-    for n in range(1, n_out):
-        start_all(down_copies(n, (w2_home + n_k * n) % n_slots))
-
-    @pl.loop(kept, n_ff)
-    def _(j):
-        wait_all(up_copies(j))
-        up_tile(j, far, 128)
-
-    @pl.loop(0, n_out)
-    def _(n):
-        base = (w2_home + n_k * n) % n_slots
-        wait_all(down_copies(n, base))
-        down_tile(n, base, far, 256)
+            start_all(down_copies(1, c1))
+            start_all(down_copies(2, c2))
+
+    start_all(down_copies(3, c3))
+    wait_all([up_slot(s) for s in range(0, 2 * n_k)])
+    for j in range(3):
+        up_tile(j, late, group, group)
+    down_tile(0, w2_home, late, group)
+    give_back(0, late)
+    down_pass([(1, c1, []), (2, c2, []), (3, c3, [])], late)
+
+    for n, base in enumerate((w2_home, c1, c2, c3)):
+        down_tile(n, base, own, 0)
+    for n in range(n_out):
+        give_back(n, own)
 
     router_copy.wait()
     w = router[...]
@@ -266,7 +292,8 @@
         c.start()
         out_copies.append(c)
     for k in range(1, N_DEV):
-        send_copy(k).wait_send()
+        if k not in (2, 4):
+            send_copy(k).wait_send()
         for n in range(n_out):
             return_copy(k, n).wait_send()
     wait_all(out_copies)
@@ -292,7 +319,7 @@
                 pltpu.VMEM((rows, d_model), BF16),
                 pltpu.VMEM((rows - CAP, d_model), BF16),
                 pltpu.VMEM((rows, d_model), BF16),
-                pltpu.VMEM((rows - 128, ff), BF16),
+                pltpu.VMEM((2 * TOK, ff), BF16),
                 pltpu.VMEM((n_slots, d_model, TN), BF16),
                 pltpu.VMEM((n_exp, TOK), F32),
                 dma((3,)), dma((n_slots,)), dma((N_DEV,)), dma((N_DEV,)),

time: 64.5 us -> 57.3 us (0.89)
  Pallas kernels: 62.5 us -> 55.2 us
    pallas_call x1, Pallas kernels: 62.5 us -> 55.2 us  [device_body(): pl.pallas_call(moe_kernel, out_shape=jax.ShapeDtypeStruct(hidden.shape, B...]
where the time goes in v3:
time: 57.3 us; the launch traced here: 57.1 us
  Pallas kernels  55.2 us (96%)
  local copies, waits for them, and re-layouts  1.88 us (3%)
    pallas_call x1, Pallas kernels, device_body(): pl.pallas_call(moe_kernel, out_shape=jax.ShapeDtypeStruct(hidden.shape, B...  55.2 us
    unnamed x1, local copies, waits for them, and re-layouts  1.88 us

profile of v3, /device:TPU:0, one launch (start us, length us, event | category | flops | bytes accessed | tf_op | source)
XLA Modules:
  0.0 57.1 jit_solution(10446984860822716585)
XLA Ops:
  0.0 55.2 %shard_map.64 = bf16[128,2048]{1,0:T(8,128)(2,1)} custom-call(bf16[128,2048]{1,0:T(8,128)(2,1)} %hid_hbm.1, f32[8,2048]{1,0:T(8,128)} %bitcast.2, s32[2,128]{1,0:T(2,128)} %bitcast.3, bf16[1,2048,5632]{2,1,0:T(8,128)(2,1)} %w1_hbm.1, bf16[1,2048,5632]{2,1,0:T(8,128)(2,1)} %w3_hbm.1, bf16[1,5632,2048]{2,1,0:T(8,128)(2,1)} %w2_hbm.1), custom_call_target="tpu_custom_call" | custom-call | tf_op jit(solution)/shard_map/pallas_call | solution.py:310
  55.3 1.9 %copy.8 = bf16[128,2048]{1,0:T(8,128)(2,1)} copy(bf16[128,2048]{1,0:T(8,128)(2,1)} %shard_map.64) | data formatting | bytes 1048576

commit v4 on v3

v4 whole, which is shorter than its diff:
```python
import functools

import jax
import jax.numpy as jnp
from jax import lax
from jax.experimental import pallas as pl
from jax.experimental.pallas import tpu as pltpu
from jax.sharding import PartitionSpec as P

MESH = pl.DeviceIdType.MESH
N_DEV = 8
CAP = 64
TOK = 128
TN = 512
VMEM_BYTES = 67043328
EXTRA = 1
SPLIT = 6
ROW_ORDER = (6, 7, 0, 1, 2, 4, 3, 5)
POS = tuple(ROW_ORDER.index(k) for k in range(N_DEV))
XS = {1: 0, 2: 1, 4: 2, 6: 3, 7: 4, 3: 0, 5: 1}
F32 = jnp.float32
BF16 = jnp.bfloat16


def peer_of(me, k):
    for bit in (1, 2, 4):
        if k & bit:
            me = me + bit - 2 * bit * ((me // bit) % 2)
    return me


def dot(a, b):
    return jnp.dot(a, b, preferred_element_type=F32)


def moe_kernel(hid_hbm, router_hbm, ids_hbm, w1_hbm, w3_hbm, w2_hbm, hid,
               router, ids, x, xsend, back, h, pool, keyt, gate,
               in_sem, pool_sem, xs_sem, xr_sem, rs_sem, rr_sem):
    me = lax.axis_index("ep")
    d_model = hid.shape[1]
    ff = h.shape[1]
    n_ff = ff // TN
    n_out = d_model // TN
    kparts = [(s, min(d_model, ff - s)) for s in range(0, ff, d_model)]
    n_k = len(kparts)
    home = [2 * n_ff + i for i in range(n_k)]
    extra = [home[-1] + 1 + i for i in range(EXTRA)]

    ids_copy = pltpu.make_async_copy(ids_hbm, ids, in_sem.at[0])
    hid_copy = pltpu.make_async_copy(hid_hbm, hid, in_sem.at[1])
    router_copy = pltpu.make_async_copy(router_hbm, router, in_sem.at[2])
    ids_copy.start()
    hid_copy.start()
    router_copy.start()

    def up_copies(j):
        cols = pl.ds(pl.multiple_of(j * TN, TN), TN)
        return (pltpu.make_async_copy(w1_hbm.at[0, :, cols], pool.at[2 * j], pool_sem.at[2 * j]),
                pltpu.make_async_copy(w3_hbm.at[0, :, cols], pool.at[2 * j + 1], pool_sem.at[2 * j + 1]))

    def down_copies(n, slots, first=0):
        cols = pl.ds(n * TN, TN)
        return [pltpu.make_async_copy(w2_hbm.at[0, pl.ds(*kparts[first + i]), cols],
                                      pool.at[p, pl.ds(0, kparts[first + i][1]), :], pool_sem.at[p])
                for i, p in enumerate(slots)]

    def start_all(copies):
        for c in copies:
            c.start()

    def wait_all(copies):
        for c in copies:
            c.wait()

    @pl.loop(0, n_ff)
    def _(j):
        start_all(up_copies(j))

    start_all(down_copies(0, home) + down_copies(1, extra))

    barrier = pltpu.get_barrier_semaphore()
    for k in range(1, N_DEV):
        pl.semaphore_signal(barrier, inc=1, device_id=(peer_of(me, k),), device_id_type=MESH)

    ids_copy.wait()
    lane = lax.broadcasted_iota(jnp.int32, (TOK, TOK), 1)
    row = lax.broadcasted_iota(jnp.int32, (TOK, TOK), 0)
    expert = lax.broadcasted_iota(jnp.int32, (N_DEV, TOK), 0)
    chosen = jnp.where((expert == ids[0:1, :]) | (expert == ids[1:2, :]), 1.0, 0.0)
    before = jnp.where(row < lane, 1.0, 0.0)
    rank = dot(chosen.astype(BF16), before.astype(BF16))
    keyt[...] = jnp.where(chosen > 0.0, rank, -1.0)
    slot = lax.broadcasted_iota(jnp.int32, (CAP, TOK), 0).astype(F32)

    def select(k):
        return jnp.where(slot == keyt[pl.ds(peer_of(me, k), 1), :], 1.0, 0.0).astype(BF16)

    def send_block(k):
        return (hid if k in (3, 5) else xsend), pl.ds(XS[k] * CAP, CAP)

    def send_copy(k):
        buf, block = send_block(k)
        return pltpu.make_async_remote_copy(
            src_ref=buf.at[block, :], dst_ref=x.at[pl.ds(POS[k] * CAP, CAP), :],
            send_sem=xs_sem.at[k], recv_sem=xr_sem.at[k], device_id=(peer_of(me, k),), device_id_type=MESH)

    def pack(ks):
        pick = jnp.concatenate([select(k) for k in ks], axis=0)
        for n in range(n_out):
            cols = pl.ds(n * TN, TN)
            rows = dot(pick, hid[:, cols]).astype(BF16)
            for i, k in enumerate(ks):
                piece = rows[i * CAP:(i + 1) * CAP]
                if k == 0:
                    x[pl.ds(POS[0] * CAP, CAP), cols] = piece
                else:
                    buf, block = send_block(k)
                    buf[block, cols] = piece

    hid_copy.wait()
    pack((2, 4))
    pl.semaphore_wait(barrier, N_DEV - 1)
    for k in (2, 4):
        send_copy(k).start()
    pack((1, 0))
    send_copy(1).start()
    pack((6, 7))

    router_copy.wait()
    w = router[...]
    w_hi = w.astype(BF16)
    rest = w - w_hi.astype(F32)
    w_mid = rest.astype(BF16)
    w_lo = (rest - w_mid.astype(F32)).astype(BF16)
    xh = hid[...]

    def logit_part(piece):
        return lax.dot_general(piece, xh, (((1,), (1,)), ((), ())), preferred_element_type=F32)

    logits = (logit_part(w_lo) + logit_part(w_mid)) + logit_part(w_hi)
    ex = jnp.exp(logits - jnp.max(logits, axis=0, keepdims=True))
    prob = ex / jnp.sum(ex, axis=0, keepdims=True)
    gates, wheres = [], []
    for c in range(2):
        hit = expert == ids[c:c + 1, :]
        gates.append(jnp.sum(jnp.where(hit, prob, 0.0), axis=0, keepdims=True))
        r = jnp.sum(jnp.where(hit, keyt[...], 0.0), axis=0, keepdims=True)
        wheres.append((ids[c:c + 1, :] ^ me).astype(F32) * float(CAP) + r)
    total = gates[0] + gates[1]
    cols4 = jnp.concatenate([gates[0] / total, gates[1] / total, wheres[0], wheres[1]]
                            + [jnp.zeros((TOK - 4, TOK), F32)], axis=0).T
    gate[...] = cols4[:, 0:N_DEV]

    pack((3, 5))

    group = 128
    far, own, near, late = 0, group, 2 * group, 3 * group

    def up_tile(j, r0, h0, rows):
        half = TN // 2
        for c in range(2):
            cols = pl.ds(c * half, half)
            u = dot(x[pl.ds(r0, rows), :], pool[2 * j, :, cols])
            v = dot(x[pl.ds(r0, rows), :], pool[2 * j + 1, :, cols])
            h[pl.ds(h0, rows), pl.ds(pl.multiple_of(j * TN + c * half, half), half)] = (
                jax.nn.silu(u) * v).astype(BF16)

    def return_copy(k, n):
        cols = pl.ds(n * TN, TN)
        return pltpu.make_async_remote_copy(
            src_ref=x.at[pl.ds(POS[k] * CAP, CAP), cols], dst_ref=back.at[pl.ds(k * CAP, CAP), cols],
            send_sem=rs_sem.at[n], recv_sem=rr_sem.at[n], device_id=(peer_of(me, k),), device_id_type=MESH)

    def returned(n):
        blocks = pl.ds(CAP, (N_DEV - 1) * CAP)
        cols = pl.ds(pl.multiple_of(n * TN, TN), TN)
        return pltpu.make_async_remote_copy(
            src_ref=x.at[blocks, cols], dst_ref=back.at[blocks, cols],
            send_sem=rs_sem.at[n], recv_sem=rr_sem.at[n], device_id=(peer_of(me, 1),), device_id_type=MESH)

    def down_tile(n, slots, r0, h0, after=None):
        cols = pl.ds(n * TN, TN)
        acc = None
        for i, (s, size) in enumerate(kparts):
            part = dot(h[pl.ds(h0, group), pl.ds(s, size)], pool[slots[i], pl.ds(0, size), :])
            acc = part if acc is None else acc + part
            if after:
                after[i].start()
        res = acc.astype(BF16)
        x[pl.ds(r0, group), cols] = res
        for i in range(group // CAP):
            k = ROW_ORDER[r0 // CAP + i]
            if k == 0:
                back[pl.ds(0, CAP), cols] = res[i * CAP:(i + 1) * CAP]

    def give_back(n, r0):
        for i in range(group // CAP):
            k = ROW_ORDER[r0 // CAP + i]
            if k:
                return_copy(k, n).start()

    send_copy(1).wait_recv()

    @pl.loop(0, SPLIT - 1)
    def _(j):
        wait_all(up_copies(j))
        up_tile(j, own, 0, group)

    for k in (2, 4):
        send_copy(k).wait_send()
    for k in (6, 7):
        send_copy(k).start()
    wait_all(up_copies(SPLIT - 1))
    up_tile(SPLIT - 1, own, 0, group)
    send_copy(2).wait_recv()
    send_copy(4).wait_recv()

    @pl.loop(SPLIT, n_ff)
    def _(j):
        wait_all(up_copies(j))
        up_tile(j, own, 0, 2 * group)

    def up_slots(slots):
        return [pltpu.make_async_copy((w3_hbm if p % 2 else w1_hbm).at[0, :, pl.ds((p // 2) * TN, TN)],
                                      pool.at[p], pool_sem.at[p]) for p in slots]

    rest = n_k - EXTRA

    def middle_copies(lent):
        return down_copies(1, lent[:rest], EXTRA) + down_copies(2, lent[rest:])

    def start_middle(lent):
        start_all(middle_copies(lent))

    def down_middle(lent, r0):
        wait_all(middle_copies(lent))
        down_tile(1, extra + lent[:rest], r0, group)
        down_tile(2, lent[rest:], r0, group)
        for n in (1, 2):
            give_back(n, r0)

    n_lent = rest + n_k
    back_c = -(-n_lent // 2)
    lent_a = list(range(2 * n_ff - n_lent, 2 * n_ff))
    lent_b = list(range(0, n_lent))
    lent_c = list(range(2 * back_c, 2 * back_c + n_lent))
    last_c = list(range(lent_c[-1] + 1, lent_c[-1] + 1 + n_k))
    start_middle(lent_a)

    @pl.loop(0, SPLIT, step=3)
    def _(j):
        for i in range(3):
            up_tile(j + i, near, group, group)

    for k in (3, 5):
        send_copy(k).start()
    wait_all(down_copies(0, home) + down_copies(1, extra))
    down_tile(0, home, near, group, down_copies(3, home))
    give_back(0, near)
    down_middle(lent_a, near)
    start_all(up_slots(lent_a))
    wait_all(down_copies(3, home))
    down_tile(3, home, near, group)
    give_back(3, near)

    send_copy(6).wait_recv()
    send_copy(7).wait_recv()
    for j in range(0, 4):
        up_tile(j, far, group, group)
    start_middle(lent_b)
    for j in range(4, 8):
        up_tile(j, far, group, group)
    wait_all(up_slots(lent_a))
    for j in range(8, n_ff):
        up_tile(j, far, group, group)
    down_tile(3, home, far, group, down_copies(0, home))
    give_back(3, far)
    down_middle(lent_b, far)
    start_all(up_slots(lent_b))
    wait_all(down_copies(0, home))
    down_tile(0, home, far, group)
    give_back(0, far)

    send_copy(3).wait_recv()
    send_copy(5).wait_recv()
    for j in range(back_c, back_c + 4):
        up_tile(j, late, group, group)
    start_middle(lent_c)
    start_all(down_copies(3, last_c))
    for j in range(back_c + 4, n_ff):
        up_tile(j, late, group, group)
    wait_all(up_slots(lent_b))
    for j in range(back_c):
        up_tile(j, late, group, group)
    down_tile(0, home, late, group)
    give_back(0, late)
    down_middle(lent_c, late)
    wait_all(down_copies(3, last_c))
    down_tile(3, last_c, late, group)
    give_back(3, late)

    own_slots = (home, extra + lent_c[:rest], lent_c[rest:], last_c)
    for n in range(2):
        down_tile(n, own_slots[n], own, 0)
    for k in range(1, N_DEV):
        if k not in (2, 4):
            send_copy(k).wait_send()
    for n in range(2, n_out):
        down_tile(n, own_slots[n], own, 0)
    for n in range(n_out):
        give_back(n, own)

    pick = xsend.at[pl.ds(0, 2 * TOK), pl.ds(0, N_DEV * CAP)]
    wide = lax.broadcasted_iota(jnp.int32, (TOK, N_DEV * CAP), 1).astype(F32)
    for c in range(2):
        pick[pl.ds(c * TOK, TOK), :] = jnp.where(wide == gate[:, 2 + c:3 + c], 1.0, 0.0).astype(BF16)

    @pl.loop(0, n_out)
    def _(n):
        cols = pl.ds(pl.multiple_of(n * TN, TN), TN)
        returned(n).wait_recv()
        both = dot(pick[...], back[:, cols])
        hid[:, cols] = (gate[:, 0:1] * both[:TOK] + gate[:, 1:2] * both[TOK:]).astype(BF16)

    @pl.loop(0, n_out)
    def _(n):
        returned(n).wait_send()


def solution(mesh):
    def device_body(hidden, w_router, ids, w_one, w_three, w_two):
        d_model, ff = w_one.shape[1:]
        n_exp = w_router.shape[1]
        rows = N_DEV * CAP
        n_out = d_model // TN
        n_slots = 2 * (ff // TN) + -(-ff // d_model) + EXTRA
        dma = pltpu.SemaphoreType.DMA
        return pl.pallas_call(
            moe_kernel,
            out_shape=pltpu.VMEM(hidden.shape, BF16),
            in_specs=[pl.BlockSpec(memory_space=pl.ANY)] * 6,
            out_specs=pl.BlockSpec(memory_space=pltpu.VMEM),
            scratch_shapes=[
                pltpu.VMEM((n_exp, d_model), F32),
                pltpu.VMEM((2, TOK), jnp.int32),
                pltpu.VMEM((rows, d_model), BF16),
                pltpu.VMEM((5 * CAP, d_model), BF16),
                pltpu.VMEM((rows, d_model), BF16),
                pltpu.VMEM((2 * TOK, ff), BF16),
                pltpu.VMEM((n_slots, d_model, TN), BF16),
                pltpu.VMEM((n_exp, TOK), F32),
                pltpu.VMEM((TOK, N_DEV), F32),
                dma((3,)), dma((n_slots,)), dma((N_DEV,)), dma((N_DEV,)),
                dma((n_out,)), dma((n_out,)),
            ],
            compiler_params=pltpu.CompilerParams(
                collective_id=0, has_side_effects=True, vmem_limit_bytes=VMEM_BYTES - 2 * hidden.size),
        )(hidden, w_router.T, ids.T, w_one, w_three, w_two)

    return jax.shard_map(
        device_body, mesh=mesh,
        in_specs=(P("ep", None), P(None, None), P("ep", None), P("ep", None, None), P("ep", None, None), P("ep", None, None)),
        out_specs=P("ep", None), check_vma=False)
```

time: 57.3 us -> 54.8 us (0.956)
  Pallas kernels: 55.2 us -> 53.9 us
  local copies, waits for them, and re-layouts: 1.88 us -> 0.8 us
    pallas_call x1, Pallas kernels: 55.2 us -> 53.9 us  [device_body(): pl.pallas_call(moe_kernel, out_shape=pltpu.VMEM(hidden.shape, BF16), in_s...]
    unnamed x1, local copies, waits for them, and re-layouts: 1.88 us -> 0.8 us
where the time goes in v4:
time: 54.8 us; the launch traced here: 54.7 us
  Pallas kernels  53.9 us (98%)
  local copies, waits for them, and re-layouts  0.8 us (1%)
    pallas_call x1, Pallas kernels, device_body(): pl.pallas_call(moe_kernel, out_shape=pltpu.VMEM(hidden.shape, BF16), in_s...  53.9 us

profile of v4, /device:TPU:0, one launch (start us, length us, event | category | flops | bytes accessed | tf_op | source)
XLA Modules:
  0.0 54.7 jit_solution(2881145311687120943)
XLA Ops:
  0.0 53.9 %shard_map.64 = bf16[128,2048]{1,0:T(8,128)(2,1)S(1)} custom-call(bf16[128,2048]{1,0:T(8,128)(2,1)} %hid_hbm.1, f32[8,2048]{1,0:T(8,128)} %bitcast.2, s32[2,128]{1,0:T(2,128)} %bitcast.3, bf16[1,2048,5632]{2,1,0:T(8,128)(2,1)} %w1_hbm.1, bf16[1,2048,5632]{2,1,0:T(8,128)(2,1)} %w3_hbm.1, bf16[1,5632,2048]{2,1,0:T(8,128)(2,1)} %w2_hbm.1), custom_call_target="tpu_custom_call" | custom-call | tf_op jit(solution)/shard_map/pallas_call | solution.py:338
  53.9 0.8 %copy.8 = bf16[128,2048]{1,0:T(8,128)(2,1)} copy(bf16[128,2048]{1,0:T(8,128)(2,1)S(1)} %shard_map.64) | data formatting | bytes 1048576

commit v5 on v4

--- a/solution.py
+++ b/solution.py
@@ -158,15 +158,16 @@
 
     def up_tile(j, r0, h0, rows):
         half = TN // 2
+        held = x[pl.ds(r0, rows), :] if rows == group else None
         for c in range(2):
             cols = pl.ds(c * half, half)
-            u = dot(x[pl.ds(r0, rows), :], pool[2 * j, :, cols])
-            v = dot(x[pl.ds(r0, rows), :], pool[2 * j + 1, :, cols])
+            u = dot(x[pl.ds(r0, rows), :] if held is None else held, pool[2 * j, :, cols])
+            v = dot(x[pl.ds(r0, rows), :] if held is None else held, pool[2 * j + 1, :, cols])
             h[pl.ds(h0, rows), pl.ds(pl.multiple_of(j * TN + c * half, half), half)] = (
                 jax.nn.silu(u) * v).astype(BF16)
 
-    def return_copy(k, n):
-        cols = pl.ds(n * TN, TN)
+    def return_copy(k, n, start=0, width=TN):
+        cols = pl.ds(n * TN + start, width)
         return pltpu.make_async_remote_copy(
             src_ref=x.at[pl.ds(POS[k] * CAP, CAP), cols], dst_ref=back.at[pl.ds(k * CAP, CAP), cols],
             send_sem=rs_sem.at[n], recv_sem=rr_sem.at[n], device_id=(peer_of(me, k),), device_id_type=MESH)
@@ -193,11 +194,11 @@
             if k == 0:
                 back[pl.ds(0, CAP), cols] = res[i * CAP:(i + 1) * CAP]
 
-    def give_back(n, r0):
+    def give_back(n, r0, start=0, width=TN):
         for i in range(group // CAP):
             k = ROW_ORDER[r0 // CAP + i]
             if k:
-                return_copy(k, n).start()
+                return_copy(k, n, start, width).start()
 
     send_copy(1).wait_recv()
 
@@ -232,8 +233,23 @@
     def start_middle(lent):
         start_all(middle_copies(lent))
 
-    def down_middle(lent, r0):
-        wait_all(middle_copies(lent))
+    def down_first(n, then, lent, r0):
+        if r0 != near:
+            wait_all(middle_copies(lent))
+        after = None if then is None else down_copies(then, home)
+        if r0 == far:
+            for start in (0, TN // 2):
+                acc = sum(dot(h[pl.ds(group, group), pl.ds(s, size)],
+                              pool[home[i], pl.ds(0, size), pl.ds(start, TN // 2)]) for i, (s, size) in enumerate(kparts))
+                x[pl.ds(r0, group), pl.ds(n * TN + start, TN // 2)] = acc.astype(BF16)
+                if start:
+                    start_all(after)
+                give_back(n, r0, start, TN // 2)
+        else:
+            down_tile(n, home, r0, group, after)
+            give_back(n, r0)
+        if r0 == near:
+            wait_all(middle_copies(lent))
         down_tile(1, extra + lent[:rest], r0, group)
         down_tile(2, lent[rest:], r0, group)
         for n in (1, 2):
@@ -247,17 +263,12 @@
     last_c = list(range(lent_c[-1] + 1, lent_c[-1] + 1 + n_k))
     start_middle(lent_a)
 
-    @pl.loop(0, SPLIT, step=3)
-    def _(j):
-        for i in range(3):
-            up_tile(j + i, near, group, group)
-
+    for j in range(SPLIT):
+        up_tile(j, near, group, group)
     for k in (3, 5):
         send_copy(k).start()
     wait_all(down_copies(0, home) + down_copies(1, extra))
-    down_tile(0, home, near, group, down_copies(3, home))
-    give_back(0, near)
-    down_middle(lent_a, near)
+    down_first(0, 3, lent_a, near)
     start_all(up_slots(lent_a))
     wait_all(down_copies(3, home))
     down_tile(3, home, near, group)
@@ -273,9 +284,7 @@
     wait_all(up_slots(lent_a))
     for j in range(8, n_ff):
         up_tile(j, far, group, group)
-    down_tile(3, home, far, group, down_copies(0, home))
-    give_back(3, far)
-    down_middle(lent_b, far)
+    down_first(3, 0, lent_b, far)
     start_all(up_slots(lent_b))
     wait_all(down_copies(0, home))
     down_tile(0, home, far, group)
@@ -292,38 +301,33 @@
     wait_all(up_slots(lent_b))
     for j in range(back_c):
         up_tile(j, late, group, group)
-    down_tile(0, home, late, group)
-    give_back(0, late)
-    down_middle(lent_c, late)
+    down_first(0, None, lent_c, late)
     wait_all(down_copies(3, last_c))
     down_tile(3, last_c, late, group)
     give_back(3, late)
 
     own_slots = (home, extra + lent_c[:rest], lent_c[rest:], last_c)
-    for n in range(2):
+    for n in range(n_out):
         down_tile(n, own_slots[n], own, 0)
+    for n in range(n_out):
+        give_back(n, own)
     for k in range(1, N_DEV):
         if k not in (2, 4):
             send_copy(k).wait_send()
-    for n in range(2, n_out):
-        down_tile(n, own_slots[n], own, 0)
-    for n in range(n_out):
-        give_back(n, own)
 
     pick = xsend.at[pl.ds(0, 2 * TOK), pl.ds(0, N_DEV * CAP)]
     wide = lax.broadcasted_iota(jnp.int32, (TOK, N_DEV * CAP), 1).astype(F32)
     for c in range(2):
         pick[pl.ds(c * TOK, TOK), :] = jnp.where(wide == gate[:, 2 + c:3 + c], 1.0, 0.0).astype(BF16)
 
-    @pl.loop(0, n_out)
-    def _(n):
-        cols = pl.ds(pl.multiple_of(n * TN, TN), TN)
-        returned(n).wait_recv()
-        both = dot(pick[...], back[:, cols])
-        hid[:, cols] = (gate[:, 0:1] * both[:TOK] + gate[:, 1:2] * both[TOK:]).astype(BF16)
-
-    @pl.loop(0, n_out)
-    def _(n):
+    for tiles in ((0, 1), (2,), (3,)):
+        for n in tiles:
+            returned(n).wait_recv()
+        for n in tiles:
+            cols = pl.ds(n * TN, TN)
+            both = dot(pick[...], back[:, cols])
+            hid[:, cols] = (gate[:, 0:1] * both[:TOK] + gate[:, 1:2] * both[TOK:]).astype(BF16)
+    for n in range(n_out):
         returned(n).wait_send()
 
 

time: 54.8 us -> 54.5 us (level)
  no operation moved by 1% of the time
where the time goes in v5:
time: 54.5 us; the launch traced here: 54.4 us
  Pallas kernels  53.6 us (98%)
  local copies, waits for them, and re-layouts  0.8 us (1%)
    pallas_call x1, Pallas kernels, device_body(): pl.pallas_call(moe_kernel, out_shape=pltpu.VMEM(hidden.shape, BF16), in_s...  53.6 us

profile of v5, /device:TPU:0, one launch (start us, length us, event | category | flops | bytes accessed | tf_op | source)
XLA Modules:
  0.0 54.4 jit_solution(14018136545177040051)
XLA Ops:
  0.0 53.6 %shard_map.64 = bf16[128,2048]{1,0:T(8,128)(2,1)S(1)} custom-call(bf16[128,2048]{1,0:T(8,128)(2,1)} %hid_hbm.1, f32[8,2048]{1,0:T(8,128)} %bitcast.2, s32[2,128]{1,0:T(2,128)} %bitcast.3, bf16[1,2048,5632]{2,1,0:T(8,128)(2,1)} %w1_hbm.1, bf16[1,2048,5632]{2,1,0:T(8,128)(2,1)} %w3_hbm.1, bf16[1,5632,2048]{2,1,0:T(8,128)(2,1)} %w2_hbm.1), custom_call_target="tpu_custom_call" | custom-call | tf_op jit(solution)/shard_map/pallas_call | solution.py:342
  53.6 0.8 %copy.8 = bf16[128,2048]{1,0:T(8,128)(2,1)} copy(bf16[128,2048]{1,0:T(8,128)(2,1)S(1)} %shard_map.64) | data formatting | bytes 1048576
